TPU v7x, 256 devices: a 4x2x16 block of a 4x16x16 slice. The times are simulated.
256 devices in a mesh: group: 2 (over y), ctx: 32 (over z, core), exp: 4 (over x).
Axes of the slice: x: 4, y: 2, z: 16, core: 2. Of those that a mesh axis runs over, the one named last changes fastest.
The devices are a block of a 4x16x16 slice.
Arguments:
- queries: bfloat16 [4096, 4096], P(('group', 'ctx'), 'exp'), parts along dimension 0, may hold values from -6 to 6
- new_keys: bfloat16 [4096, 1024], P(('group', 'ctx'), 'exp'), parts along dimension 0, may hold values from -6 to 6
- new_values: bfloat16 [4096, 1024], P(('group', 'ctx'), 'exp'), parts along dimension 0, may hold values from -6 to 6
- cache_keys: bfloat16 [16384, 1024], P(('group', 'ctx'), 'exp'), parts along dimension 0, may hold values from -6 to 6
- cache_values: bfloat16 [16384, 1024], P(('group', 'ctx'), 'exp'), parts along dimension 0, may hold values from -6 to 6
- offset: int32 [2], P('group'), parts along dimension 0, may hold values from 4096 to 8192
- token_ids: int32 [4096], P(('group', 'ctx')), parts along dimension 0, may hold values from 0 to 128255, as said below
- expert_table: int32 [256512], P('group'), parts along dimension 0, may hold values from 0 to 3
- norm_gain: float32 [4096], replicated, may hold values from 0.5 to 1.5
- w_gate: bfloat16 [4, 4096, 14336], P('exp', None, 'ctx'), may hold values from -0.09375 to 0.09375
- w_up: bfloat16 [4, 4096, 14336], P('exp', None, 'ctx'), may hold values from -0.09375 to 0.09375
- w_down: bfloat16 [4, 14336, 4096], P('exp', 'ctx'), may hold values from -0.046875 to 0.046875
Outputs:
- mixed: bfloat16 [4096, 4096], P(('group', 'ctx'), 'exp'), parts along dimension 0
There are 2 independent parts, one for each index of `group`. A program takes and returns all parts, laid end to end along the dimension named above; an argument that names none is the same for every part. Nothing has to cross between parts.
Inputs may be any that keep to these rules, and one draw needn't show every extreme that they name: Cache positions at or beyond offset are not yet filled. `token_ids`: in every block of 64 consecutive stretch tokens (one block per index of ctx) at most 32 tokens map to one expert through expert_table, and one expert takes exactly 32 tokens of every block.
All inputs are finite; a program needn't handle non-finite values.
Results may differ from a plain program's by a relative error of at most 0.025.
Values may be sent and summed in bfloat16 or wider, within the bound.
A program may use at most 128 MiB of HBM per device.

v0:
```python
import math

import jax
import jax.numpy as jnp
from jax import lax
from jax.sharding import Mesh
from jax.sharding import PartitionSpec as P

HEADS = 32
KV_HEADS = 8
HEAD_DIM = 128
CTX = ("ctx_0", "ctx_1")
GROUP_CTX = ("group", "ctx_0", "ctx_1")


masked_score = -1e30


def sent_together(arrays, axis, dim, along):
    widths = [a.shape[along] for a in arrays]
    both = jnp.concatenate(arrays, axis=along)
    filled = lax.all_gather(both, axis, axis=dim, tiled=True)
    return tuple(jnp.split(filled, [sum(widths[:k]) for k in range(1, len(widths))], axis=along))


def own_block(tiles, axes, order):
    shape = [lax.axis_size(a) for a in axes]
    tiles = tiles.reshape(*shape, *tiles.shape[1:])
    tiles = tiles.transpose(*order, *range(len(axes), tiles.ndim))
    tiles = tiles.reshape(-1, *tiles.shape[len(axes) :])
    for k in order:
        tiles = lax.psum_scatter(tiles, axes[k], scatter_dimension=0, tiled=True)
    return tiles[0]


def in_blocks(array, dim, devices):
    shape = array.shape
    tiles = array.reshape(*shape[:dim], devices, shape[dim] // devices, *shape[dim + 1 :])
    return jnp.moveaxis(tiles, dim, 0)


def summed_rows(array, axes, order, dim):
    devices = lax.axis_size(axes)
    return own_block(in_blocks(array, dim, devices), axes, order)


def split_heads(flat, heads):
    return flat.reshape(flat.shape[0], heads, flat.shape[1] // heads)


def partial_attend(query_rows, key_rows, value_rows, allowed):
    width = query_rows.shape[3]
    scores = jnp.einsum("rkgd,skd->rkgs", query_rows, key_rows, preferred_element_type=jnp.float32)
    scores = scores * (1.0 / math.sqrt(width))
    usable = allowed[:, None, None, :]
    peak = jnp.max(jnp.where(usable, scores, masked_score), axis=-1)
    unnorm = jnp.where(usable, jnp.exp(scores - peak[..., None]), 0.0)
    total = jnp.sum(unnorm, axis=-1)
    numer = jnp.einsum(
        "rkgs,skd->rkgd",
        unnorm.astype(jnp.bfloat16),
        value_rows,
        preferred_element_type=jnp.float32,
    )
    return (numer, peak, total)


def on_device(
    queries,
    new_keys,
    new_values,
    cache_keys,
    cache_values,
    offset,
    token_ids,
    expert_table,
    norm_gain,
    w_gate,
    w_up,
    w_down,
):
    owners = lax.axis_size("exp")
    heads_local = HEADS // owners
    kv_local = KV_HEADS // owners
    group = HEADS // KV_HEADS
    tok_count = queries.shape[0]
    cache_len = cache_keys.shape[0]
    shard = lax.axis_index(CTX)
    limit = offset[0]
    key_rows = jnp.concatenate([cache_keys, new_keys], axis=0)
    value_rows = jnp.concatenate([cache_values, new_values], axis=0)
    span = key_rows.shape[0]
    own_index = shard * tok_count + jnp.arange(tok_count, dtype=jnp.int32)
    grouped = queries.reshape(tok_count, kv_local, group, HEAD_DIM)
    piece_keys, piece_values = sent_together((key_rows, value_rows), CTX, 0, 1)
    flat = jnp.arange(piece_keys.shape[0], dtype=jnp.int32)
    source = flat // span
    inner = flat % span
    cache_ok = source * cache_len + inner < limit
    stretch_ok = (source * tok_count + inner - cache_len)[None, :] <= own_index[:, None]
    allowed = jnp.where((inner < cache_len)[None, :], cache_ok[None, :], stretch_ok)
    numer, peak, total = partial_attend(
        grouped, split_heads(piece_keys, kv_local), split_heads(piece_values, kv_local), allowed
    )
    best = jnp.full((tok_count, kv_local, group), masked_score, jnp.float32)
    higher = jnp.maximum(best, peak)
    fresh = jnp.exp(peak - higher)
    accum = numer * fresh[..., None]
    denom = total * fresh
    attended = (
        (accum / denom[..., None]).reshape(tok_count, heads_local * HEAD_DIM).astype(jnp.bfloat16)
    )
    capacity = tok_count // 2
    chosen = expert_table[token_ids]
    onehot = (chosen[:, None] == jnp.arange(owners, dtype=jnp.int32)[None, :]).astype(jnp.int32)
    earlier = jnp.cumsum(onehot, axis=0) - onehot
    slot = jnp.sum(earlier * onehot, axis=1)
    target = chosen * capacity + slot
    dispatch = (jnp.arange(owners * capacity, dtype=jnp.int32)[:, None] == target[None, :]).astype(
        jnp.bfloat16
    )
    packed = jnp.dot(dispatch, attended, preferred_element_type=jnp.float32).astype(jnp.bfloat16)
    arrived = lax.all_to_all(packed, "exp", split_axis=0, concat_axis=1, tiled=True)
    values32 = arrived.astype(jnp.float32)
    scale = lax.rsqrt(jnp.mean(values32 * values32, axis=-1, keepdims=True) + 1e-05)
    normed = (values32 * scale * norm_gain).astype(jnp.bfloat16)
    gate_w = w_gate[0]
    up_w = w_up[0]
    down_w = w_down[0]
    piece = lax.all_gather(normed, CTX, axis=0, tiled=True)
    gate = jnp.dot(piece, gate_w, preferred_element_type=jnp.float32)
    upper = jnp.dot(piece, up_w, preferred_element_type=jnp.float32)
    hidden = (jax.nn.silu(gate) * upper).astype(jnp.bfloat16)
    summed = summed_rows(
        jnp.dot(hidden, down_w, preferred_element_type=jnp.float32).astype(jnp.bfloat16),
        CTX,
        (1, 0),
        0,
    ).astype(jnp.float32)
    combined = (normed.astype(jnp.float32) + summed).astype(jnp.bfloat16)
    returned = lax.all_to_all(combined, "exp", split_axis=1, concat_axis=0, tiled=True)
    collect = (target[:, None] == jnp.arange(owners * capacity, dtype=jnp.int32)[None, :]).astype(
        jnp.bfloat16
    )
    return jnp.dot(collect, returned, preferred_element_type=jnp.float32).astype(jnp.bfloat16)


def solution(mesh):
    torus = Mesh(
        mesh.devices.reshape(mesh.shape["group"], 16, 2, mesh.shape["exp"]),
        ("group", "ctx_0", "ctx_1", "exp"),
    )
    placed = (
        P(GROUP_CTX, "exp"),
        P(GROUP_CTX, "exp"),
        P(GROUP_CTX, "exp"),
        P(GROUP_CTX, "exp"),
        P(GROUP_CTX, "exp"),
        P("group"),
        P(GROUP_CTX),
        P("group"),
        P(),
        P("exp", None, CTX),
        P("exp", None, CTX),
        P("exp", CTX, None),
    )
    return jax.shard_map(
        on_device, mesh=torus, in_specs=placed, out_specs=P(GROUP_CTX, "exp"), check_vma=False
    )
```

profile of v0, /device:TPU:40, one launch (start us, length us, event | category | flops | bytes accessed | tf_op | source)
XLA Modules:
  0.0 400.0 jit_solution(10660511344860597699)
XLA Ops:
  6.6 1.8 maximum_maximum_fusion
  9.2 1.0 reshape.150
  10.1 0.7 compare_select_fusion.1
  10.8 0.8 gather_fusion
  12.0 0.5 compare_select_fusion
  12.6 89.4 %all-gather.3.cloned.1.call-done = bf16[10240,512]{1,0:T(8,128)(2,1)} async-done(((bf16[320,512]{1,0:T(8,128)(2,1)}), bf16[10240,512]{1,0:T(8,128)(2,1)}) %all-gather.3.cloned.1.call-update) | async-done | bytes 10485776 | tf_op jit(solution)/shard_map/all_gather | solution.py:22
  102.0 8.9 %fusion.47 = (bf16[10240,256]{1,0:T(8,128)(2,1)}, bf16[10240,256]{1,0:T(8,128)(2,1)}) fusion(bf16[10240,512]{1,0:T(8,128)(2,1)} %all-gather.3.cloned.1.call-done), kind=kLoop, calls=%fused_computation.65 | loop fusion | bytes 20971520 | tf_op jit(solution)/shard_map/split | solution.py:23
  110.9 7.9 %copy.50 = bf16[10240,256]{0,1:T(8,128)(2,1)} copy(bf16[10240,256]{1,0:T(8,128)(2,1)} %get-tuple-element.6) | data formatting | bytes 10485760
  118.8 8.0 %copy.51 = bf16[10240,256]{0,1:T(8,128)(2,1)} copy(bf16[10240,256]{1,0:T(8,128)(2,1)} %get-tuple-element.5) | data formatting | bytes 10485760
  126.7 12.0 %fusion = (f32[64,2,4]{0,2,1:T(4,128)S(1)}, f32[2,10240,64,4]{1,2,3,0:T(8,128)}) fusion(pred[64,10240]{1,0:T(8,128)(4,1)S(1)} %compare_select_fusion, bf16[10240,2,128,1]{0,2,3,1:T(8,128)(2,1)} %bitcast.77, bf16[64,2,4,128]{3,2,1,0:T(4,128)(2,1)S(1)} %reshape.150), kind=kOutput, calls=%fused_computation.3 | convolution fusion | flops 1357905408 | bytes 27002880 | tf_op jit(solution)/shard_map/rkgd,skd->rkgs/dot_general | solution.py:53
  138.7 10.0 %fusion.3 = f32[64,2,4]{0,2,1:T(4,128)S(1)} fusion(f32[2,10240,64,4]{1,2,3,0:T(8,128)} %get-tuple-element.10, f32[64,2,4]{0,2,1:T(4,128)S(1)} %get-tuple-element.9, pred[64,10240]{1,0:T(8,128)(4,1)S(1)} %compare_select_fusion), kind=kLoop, calls=%fused_computation.6 | loop fusion | flops 20971008 | bytes 21630976 | tf_op jit(solution)/shard_map/reduce_sum | solution.py:58
  148.7 10.6 %fusion.26 = bf16[64,2,4,128]{3,0,2,1:T(8,128)(2,1)S(1)} fusion(bf16[10240,2,128,1]{0,2,3,1:T(8,128)(2,1)} %bitcast.79, f32[2,10240,64,4]{1,2,3,0:T(8,128)} %get-tuple-element.10, f32[64,2,4]{0,2,1:T(4,128)S(1)} %get-tuple-element.9, pred[64,10240]{1,0:T(8,128)(4,1)S(1)} %compare_select_fusion, f32[64,2,4]{0,2,1:T(4,128)S(1)} %get-tuple-element.8, ...), kind=kOutput, calls=%fused_computation.23 | convolution fusion | flops 1363345408 | bytes 27006976 | tf_op jit(solution)/shard_map/rkgs,skd->rkgd/dot_general | solution.py:59
  159.8 11.1 %all_to_all.29 = bf16[4,32,1024]{2,1,0:T(8,128)(2,1)S(1)} all-to-all(bf16[4,32,1024]{2,1,0:T(8,128)(2,1)S(1)} %bitcast.83), channel_id=1, replica_groups=mesh['group'=2,'ctx_0'=16,'ctx_1'=2,'exp'=4] {'exp'}, dimensions={0} | all-to-all | bytes 524288 | tf_op jit(solution)/shard_map/all_to_all | solution.py:123
  171.4 0.4 multiply_reduce_fusion
  171.8 0.8 multiply_convert_fusion.1
  172.9 71.4 %all-gather.5.cloned.1.call-done = bf16[1024,4096]{1,0:T(8,128)(2,1)} async-done(((bf16[32,4096]{1,0:T(8,128)(2,1)}), bf16[1024,4096]{1,0:T(8,128)(2,1)}) %all-gather.5.cloned.1.call-update) | async-done | bytes 8388624 | tf_op jit(solution)/shard_map/all_gather | solution.py:130
  244.3 7.5 %fusion.11 = f32[1024,448]{0,1:T(8,128)S(1)} fusion(bf16[1024,4096]{1,0:T(8,128)(2,1)} %all-gather.5.cloned.1.call-done, bf16[1,4096,448]{1,2,0:T(8,128)(2,1)} %param.21), kind=kOutput, calls=%fused_computation.14 | convolution fusion | flops 3758096384 | bytes 13893632 | tf_op jit(solution)/shard_map/dot_general | solution.py:131
  251.8 15.2 %convolution_convert_fusion = bf16[1024,4096]{1,0:T(8,128)(2,1)} fusion(bf16[1,448,4096]{2,1,0:T(8,128)(2,1)} %param.23, f32[1024,448]{0,1:T(8,128)S(1)} %fusion.11, bf16[1024,4096]{1,0:T(8,128)(2,1)} %all-gather.5.cloned.1.call-done, bf16[1,4096,448]{1,2,0:T(8,128)(2,1)} %param.22), kind=kOutput, calls=%fused_computation.10 | convolution fusion | flops 7523139584 | bytes 25952256 | tf_op jit(solution)/shard_map/dot_general | solution.py:135
  267.0 7.7 %copy.42 = bf16[16,2,32,4096]{3,2,0,1:T(8,128)(2,1)} copy(bf16[16,2,32,4096]{3,2,1,0:T(8,128)(2,1)} %bitcast.78) | data formatting | bytes 16777216 | tf_op jit(solution)/shard_map/reshape;reshape | solution.py:28
  274.9 22.1 %reduce-scatter.3.cloned.1.call-done = bf16[16,32,4096]{2,1,0:T(8,128)(2,1)} async-done(((bf16[32,32,4096]{2,1,0:T(8,128)(2,1)}), bf16[16,32,4096]{2,1,0:T(8,128)(2,1)}) %reduce-scatter.3.cloned.1.call-update) | async-done | bytes 4194320 | tf_op jit(solution)/shard_map/reduce_scatter | solution.py:32
  297.1 82.6 %reduce-scatter.5.cloned.1.call-done = bf16[1,32,4096]{2,1,0:T(8,128)(2,1)} async-done(((bf16[16,32,4096]{2,1,0:T(8,128)(2,1)}), bf16[1,32,4096]{2,1,0:T(8,128)(2,1)}) %reduce-scatter.5.cloned.1.call-update) | async-done | bytes 262160 | tf_op jit(solution)/shard_map/reduce_scatter | solution.py:32
  379.7 1.4 reshape.153
  381.4 11.2 %all_to_all.30 = bf16[32,4,1024]{2,0,1:T(8,128)(2,1)S(1)} all-to-all(bf16[32,4,1024]{2,0,1:T(8,128)(2,1)S(1)} %copy.43), channel_id=1, replica_groups=mesh['group'=2,'ctx_0'=16,'ctx_1'=2,'exp'=4] {'exp'}, dimensions={1} | all-to-all | bytes 524288 | tf_op jit(solution)/shard_map/all_to_all | solution.py:141
  392.6 0.9 convolution_convert_fusion.2
  (32 shorter events, 2.3 us)
Async XLA Ops:
  6.5 4.3 %copy-start = (s32[128256]{0:T(1024)S(1)}, s32[128256]{0:T(1024)}, u32[]{:S(2)}) copy-start(s32[128256]{0:T(1024)} %param.19) | copy-start | bytes 1539076
  6.6 95.5 %all-gather.3.cloned.1.call-start = ((), (), s32[]{:S(2)}) async-start(), calls=%async_computation.4 | async-start | bytes 10813440 | tf_op jit(solution)/shard_map/all_gather | solution.py:22
  8.4 235.9 %all-gather.5.cloned.1.call-start = ((), (), s32[]{:S(2)}) async-start(), calls=%async_computation.5 | async-start | bytes 8650752 | tf_op jit(solution)/shard_map/all_gather | solution.py:130
  148.7 23.0 %copy-start.2 = (f32[4096]{0:T(1024)S(1)}, f32[4096]{0:T(1024)}, u32[]{:S(2)}) copy-start(f32[4096]{0:T(1024)} %param.20) | copy-start | bytes 49156
  172.7 124.3 %reduce-scatter.3.cloned.1.call-start = ((), (), s32[]{:S(2)}) async-start(), calls=%async_computation.6 | async-start | bytes 12582912 | tf_op jit(solution)/shard_map/reduce_scatter | solution.py:32
  274.8 118.7 %copy-start.1 = (s32[128256]{0:T(1024)S(1)}, s32[128256]{0:T(1024)}, u32[]{:S(2)}) copy-start(s32[128256]{0:T(1024)} %param.19) | copy-start | bytes 1539076
  274.8 104.9 %reduce-scatter.5.cloned.1.call-start = ((), (), s32[]{:S(2)}) async-start(), calls=%async_computation.7 | async-start | bytes 4456448 | tf_op jit(solution)/shard_map/reduce_scatter | solution.py:32
Sparse Core Ops, SparseCore 0:
  9.2 92.7 all-gather.2
  172.8 71.4 all-gather.4
  274.9 22.0 reduce-scatter.2
  299.4 80.2 reduce-scatter.4
where the time goes:
time: 401 us; the launch traced here: 400 us
  waiting for transfers between devices  266 us (66%)
  matrix products  46.4 us (12%)
  local copies, waits for them, and re-layouts  36.1 us (9%)
  blocking collectives  22.3 us (6%)
  other arithmetic  15.2 us (4%)
  between operations  13.9 us (3%)
    reduce_scatter x2, waiting for transfers between devices, own_block(): tiles = lax.psum_scatter(tiles, axes[k], scatter_dimension=0, tiled=True)  105 us
    all_gather x1, waiting for transfers between devices, sent_together(): filled = lax.all_gather(both, axis, axis=dim, tiled=True)  89.4 us
    all_gather x1, waiting for transfers between devices, on_device(): piece = lax.all_gather(normed, CTX, axis=0, tiled=True)  71.4 us
    unnamed x9, local copies, waits for them, and re-layouts  16.2 us
    dot_general x1, matrix products, on_device(): jnp.dot(hidden, down_w, preferred_element_type=jnp.float32)  15.2 us
    dot_general x1, matrix products, partial_attend(): jnp.einsum('rkgd,skd->rkgs', query_rows, key_rows, preferred_element_type...  12 us
    all_to_all x1, blocking collectives, on_device(): lax.all_to_all(combined, 'exp', split_axis=1, concat_axis=0, tiled=True)  11.2 us
    all_to_all x1, blocking collectives, on_device(): lax.all_to_all(packed, 'exp', split_axis=0, concat_axis=1, tiled=True)  11.1 us
  transfers between devices with their start and end apart: 4, of which 4 were waited for; matrix products, arithmetic and copies ran while one was open for 1% of the time, Pallas kernels for 0%

commit v1 on v0

v1 whole, which is shorter than its diff:
```python
import functools
import math

import jax
import jax.numpy as jnp
from jax import lax
from jax.experimental import pallas as pl
from jax.experimental.pallas import tpu as pltpu
from jax.sharding import PartitionSpec as P

MESH = pl.DeviceIdType.MESH
F32 = jnp.float32
BF16 = jnp.bfloat16
HEAD = 128
NEG = -1e30
VMEM_LIMIT = 64000 * 1024


def layer_kernel(
    nz,
    nx,
    offset_ref,
    q_hbm,
    nk_hbm,
    nv_hbm,
    ck_hbm,
    cv_hbm,
    disp_hbm,
    coll_ref,
    gain_ref,
    wg_hbm,
    wu_hbm,
    wd_hbm,
    out_ref,
    kbuf,
    vbuf,
    qbuf,
    qcat,
    dbuf,
    tok_ref,
    m_ref,
    l_ref,
    o_ref,
    att,
    packed,
    arr,
    rows,
    sums,
    rsb,
    gate_s,
    hid,
    comb,
    ret,
    wg,
    wu,
    wd,
    loc_sem,
    pair_send,
    pair_recv,
    w_loc,
    w_send,
    w_recv,
    kv_send,
    kv_recv,
    a_send,
    a_recv,
    g_send,
    g_recv,
    r_send,
    r_recv,
    b_send,
    b_recv,
):
    ctx = lax.axis_index("ctx")
    x = lax.axis_index("exp")
    z = ctx // 2
    c = ctx % 2
    oc = 1 - c
    half = nz // 2
    right = {"ctx": ((z + 1) % nz) * 2 + c, "exp": x}
    left = {"ctx": ((z + nz - 1) % nz) * 2 + c, "exp": x}
    ahead = (right, left)
    pair = {"ctx": z * 2 + oc, "exp": x}
    T = q_hbm.shape[0]
    CK = ck_hbm.shape[0]
    NK = nk_hbm.shape[0]
    QW = qbuf.shape[2]
    group = QW // HEAD
    cap = arr.shape[0]
    width = arr.shape[1]
    hrow = cap // 2
    hcol = width // 2

    def remote(src, dst, ssem, rsem, dev):
        return pltpu.make_async_remote_copy(
            src_ref=src, dst_ref=dst, send_sem=ssem, recv_sem=rsem, device_id=dev, device_id_type=MESH
        )

    kcol = pl.ds(pl.multiple_of(c * HEAD, HEAD), HEAD)
    kcol_o = pl.ds(pl.multiple_of(oc * HEAD, HEAD), HEAD)
    qcol = pl.ds(pl.multiple_of(c * QW, HEAD), QW)
    qcol_o = pl.ds(pl.multiple_of(oc * QW, HEAD), QW)
    parts = (
        (ck_hbm, kbuf, 0, CK),
        (nk_hbm, kbuf, CK, NK),
        (cv_hbm, vbuf, 0, CK),
        (nv_hbm, vbuf, CK, NK),
    )
    local = []
    for i, (src, buf, lo, n) in enumerate(parts):
        local.append(
            pltpu.make_async_copy(src.at[:, kcol], buf.at[0, 0, pl.ds(lo, n), :], loc_sem.at[i])
        )
    local.append(pltpu.make_async_copy(q_hbm.at[:, qcol], qbuf.at[0], loc_sem.at[4]))
    local.append(pltpu.make_async_copy(disp_hbm, dbuf.at[0], loc_sem.at[5]))
    for cp in local:
        cp.start()

    barrier = pltpu.get_barrier_semaphore()
    others = []
    for d in range(nx):
        for k in range(2):
            if d or k:
                others.append((d, k))
    for dev in ahead:
        pl.semaphore_signal(barrier, inc=1, device_id=dev, device_id_type=MESH)
    for d, k in others:
        pl.semaphore_signal(
            barrier,
            inc=1,
            device_id={"ctx": z * 2 + (c + k) % 2, "exp": (x + d) % nx},
            device_id_type=MESH,
        )
    pl.semaphore_wait(barrier, 2 + len(others))

    swap = []
    for i, (src, buf, lo, n) in enumerate(parts):
        swap.append(
            remote(src.at[:, kcol_o], buf.at[0, 1, pl.ds(lo, n), :], pair_send.at[i], pair_recv.at[i], pair)
        )
    swap.append(remote(q_hbm.at[:, qcol_o], qbuf.at[1], pair_send.at[4], pair_recv.at[4], pair))
    swap.append(remote(disp_hbm, dbuf.at[1], pair_send.at[5], pair_recv.at[5], pair))
    for cp in swap:
        cp.start()

    def last_pos(d, s):
        return 2 * s - 1 if d == 0 else 2 * s - s // half

    def kv_chunk(k, pos):
        return (kbuf, vbuf)[k % 2].at[pos, k // 2]

    def kv_copy(d, k, s, pos):
        return remote(
            kv_chunk(k, pos),
            kv_chunk(k, last_pos(d, s)),
            kv_send.at[d, k],
            kv_recv.at[d, s - 1, k],
            ahead[d],
        )

    for i in range(4):
        local[i].wait()
    for k in (0, 1):
        for d in (0, 1):
            kv_copy(d, k, 1, 0).start()
    local[4].wait()
    local[5].wait()
    for i in range(4):
        swap[i].wait_recv()
    for k in (2, 3):
        for d in (0, 1):
            kv_copy(d, k, 1, 0).start()

    weights = ((wg_hbm, wg), (wu_hbm, wu), (wd_hbm, wd))
    w_own = [pltpu.make_async_copy(src.at[0], dst.at[0], w_loc.at[i]) for i, (src, dst) in enumerate(weights)]
    w_swap = [remote(src.at[0], dst.at[1], w_send.at[i], w_recv.at[i], pair) for i, (src, dst) in enumerate(weights)]
    for cp in w_own:
        cp.start()
    for cp in w_swap:
        cp.start()

    swap[4].wait_recv()
    swap[5].wait_recv()
    for g in range(group):
        for s in range(2):
            qcat[pl.ds((g * 2 + s) * T, T), :] = qbuf[s, :, pl.ds(g * HEAD, HEAD)]
    lanes = 2 * T * group
    lane = lax.broadcasted_iota(jnp.int32, (1, lanes), 1)
    bits = T.bit_length() - 1
    second = lax.shift_right_logical(lane, bits) & 1
    tok_ref[...] = z * (2 * T) + (lane & (T - 1)) + jnp.where(second == 0, c, oc) * T
    m_ref[...] = jnp.full_like(m_ref, NEG)
    l_ref[...] = jnp.zeros_like(l_ref)
    o_ref[...] = jnp.zeros_like(o_ref)
    scale = 1.0 / math.sqrt(HEAD)
    nt = (((1,), (1,)), ((), ()))
    tn = (((0,), (0,)), ((), ()))

    def attend(pos, src, zz):
        owner = zz * 2 + (c if src == 0 else oc)
        s = lax.dot_general(kbuf[pos, src], qcat[...], nt, preferred_element_type=F32) * scale
        crow = lax.broadcasted_iota(jnp.int32, (CK, 1), 0) + owner * CK
        sc = jnp.where(crow < offset_ref[0], s[:CK], NEG)
        nrow = lax.broadcasted_iota(jnp.int32, (NK, lanes), 0) + owner * NK
        sn = jnp.where(nrow <= tok_ref[...], s[CK:], NEG)
        m_old = m_ref[...]
        m_new = jnp.maximum(
            m_old,
            jnp.maximum(jnp.max(sc, axis=0, keepdims=True), jnp.max(sn, axis=0, keepdims=True)),
        )
        pc = jnp.exp(sc - m_new)
        pn = jnp.exp(sn - m_new)
        fade = jnp.exp(m_old - m_new)
        m_ref[...] = m_new
        l_ref[...] = (
            l_ref[...] * fade + jnp.sum(pc, axis=0, keepdims=True) + jnp.sum(pn, axis=0, keepdims=True)
        )
        p = jnp.concatenate([pc.astype(BF16), pn.astype(BF16)], axis=0)
        o_ref[...] = o_ref[...] * fade + lax.dot_general(vbuf[pos, src], p, tn, preferred_element_type=F32)

    def kv_step(s, carry):
        for k in range(4):
            for d in (0, 1):
                here = last_pos(d, s)
                kv_copy(d, k, s, here).wait_recv()
                onward = kv_copy(d, k, s + 1, here)
                if k // 2 == d:
                    onward.wait_send()
                    onward.start()
                else:

                    @pl.when(s < half - 1)
                    def _():
                        onward.wait_send()
                        onward.start()

            if k < 2:

                @pl.when(s > 1)
                def _():
                    attend(2 * s - 3, k, (z + nz - s + 1) % nz)

            else:
                attend(2 * s - 2, k - 2, (z + s - 1) % nz)
        return carry

    lax.fori_loop(1, half, kv_step, 0)
    for k in range(2):
        attend(2 * half - 3, k, (z + nz - half + 1) % nz)
    for k in range(2):
        attend(2 * half - 2, k, (z + half - 1) % nz)
    for d in (0, 1):
        for k in (2 * d, 2 * d + 1):
            kv_copy(d, k, half, 2 * half - 1).wait_recv()
        attend(2 * half - 1, d, (z + half) % nz)
    for k in range(4):
        for d in (0, 1):
            kv_copy(d, k, half, 0).wait_send()
    for cp in swap:
        cp.wait_send()

    done = o_ref[...] / l_ref[...]
    for g in range(group):
        att[:, pl.ds(g * HEAD, HEAD)] = done[:, g * 2 * T : (g + 1) * 2 * T].T.astype(BF16)
    for k in range(2):
        packed[k] = jnp.dot(
            dbuf[k, :, pl.ds(0, T)], att[pl.ds(k * T, T), :], preferred_element_type=F32
        ).astype(BF16)

    mine = pl.ds(pl.multiple_of((x * 2 + c) * QW, HEAD), QW)

    def slots(e):
        return pl.ds(pl.multiple_of(e * cap, cap), cap)

    there = []
    for d, k in others:
        e = (x + d) % nx
        there.append(
            remote(
                packed.at[k, slots(e), :],
                arr.at[:, mine],
                a_send.at[d, k],
                a_recv.at[d, k],
                {"ctx": z * 2 + (c + k) % 2, "exp": e},
            )
        )
    for cp in there:
        cp.start()
    arr[:, mine] = packed[0, slots(x), :]
    for cp in there:
        cp.wait_recv()
    v32 = arr[...].astype(F32)
    norm = lax.rsqrt(jnp.mean(v32 * v32, axis=-1, keepdims=True) + 1e-05)
    rows[pl.ds(0, cap), :] = (v32 * norm * gain_ref[...]).astype(BF16)

    def part(ref, pos, k):
        return ref.at[
            pl.ds(pl.multiple_of(pos * cap + (k // 2) * hrow, hrow), hrow), pl.ds((k % 2) * hcol, hcol)
        ]

    def row_copy(d, k, s, pos):
        return remote(
            part(rows, pos, k),
            part(rows, last_pos(d, s), k),
            g_send.at[d, k],
            g_recv.at[d, s - 1, k],
            ahead[d],
        )

    for k in range(4):
        for d in (0, 1):
            row_copy(d, k, 1, 0).start()
    for cp in there:
        cp.wait_send()
    for cp in w_own:
        cp.wait()
    for cp in w_swap:
        cp.wait()

    M = 4 * cap
    ncols = 4
    ncol = width // ncols

    def dense(g, i):
        lo = pl.multiple_of(g * M, M)
        if i < 4:
            src = i // 2
            w = (wg, wu)[i % 2]
            v = jnp.dot(rows[pl.ds(lo, M), :], w[src], preferred_element_type=F32)
            if i % 2 == 0:
                gate_s[...] = v
            else:
                g32 = gate_s[...]
                hid[src] = (g32 / (1.0 + jnp.exp(-g32)) * v).astype(BF16)
        else:
            cols = pl.ds((i - 4) * ncol, ncol)
            sums[pl.ds(lo, M), cols] = (
                jnp.dot(hid[0], wd[0, :, cols], preferred_element_type=F32)
                + jnp.dot(hid[1], wd[1, :, cols], preferred_element_type=F32)
            ).astype(BF16)

    pairs = half // 2

    def row_pair(j, carry):
        more = j < pairs - 1
        for o in range(2):
            s = 2 * j + 1 + o
            for k in range(4):
                for d in (0, 1):
                    here = last_pos(d, s)
                    arrive = row_copy(d, k, s, here)
                    onward = row_copy(d, k, s + 1, here)
                    keep = k // 2 == d

                    def on():
                        onward.wait_send()
                        onward.start()

                    if o == 0:
                        arrive.wait_recv()
                        if keep:
                            on()
                        else:
                            pl.when(more)(on)
                    elif keep:
                        arrive.wait_recv()
                        pl.when(more)(on)
                    else:

                        @pl.when(more)
                        def _():
                            arrive.wait_recv()
                            on()

                @pl.when(j > 0)
                def _():
                    dense(j - 1, o * 4 + k)

        return carry

    lax.fori_loop(0, pairs, row_pair, 0)
    for k in range(4):
        for d in (0, 1):
            row_copy(d, k, half, 0).wait_send()

    def sum_copy(d, k, s):
        pos = 2 * s - s // half if d == 0 else 2 * s - 1
        return remote(
            part(sums, pos, k),
            part(rsb.at[d], s - 1, k),
            r_send.at[d, k],
            r_recv.at[d, s - 1, k],
            ahead[d],
        )

    for i in range(8):
        dense(pairs - 1, i)
    for q in range(2):
        for d in (0, 1):
            sum_copy(d, 2 * d + q, half).start()

    def add_in(d, k, s):
        pos = 2 * s if d == 0 else 2 * s - 1
        sum_copy(d, k, s + 1).wait_recv()
        own = part(sums, pos, k)
        own[...] = (own[...].astype(F32) + part(rsb.at[d], s, k)[...].astype(F32)).astype(BF16)

    def sum_step(t, carry):
        s = half - 1 - t
        for q in range(2):
            for d in (0, 1):
                k = 2 * (1 - d) + q

                @pl.when(t > 0)
                def _():
                    add_in(d, k, s)
                    sum_copy(d, k, s).wait_send()

                sum_copy(d, k, s).start()
        for q in range(2):
            for d in (0, 1):
                k = 2 * d + q
                add_in(d, k, s)
                sum_copy(d, k, s).wait_send()
                sum_copy(d, k, s).start()
        return carry

    lax.fori_loop(0, half - 1, sum_step, 0)

    for h in range(2):
        for q in range(2):
            k = 2 * h + q
            for d in (0, 1):
                sum_copy(d, k, 1).wait_recv()
            total = part(rows, 0, k)[...].astype(F32) + (
                part(sums, 0, k)[...].astype(F32)
                + part(rsb.at[0], 0, k)[...].astype(F32)
                + part(rsb.at[1], 0, k)[...].astype(F32)
            )
            part(comb, 0, k)[...] = total.astype(BF16)
    tw = width // nx

    def cols_of(e):
        return pl.ds(pl.multiple_of(e * tw, HEAD), tw)

    back = []
    for d in range(1, nx):
        e = (x + d) % nx
        back.append(
            remote(
                comb.at[:, cols_of(e)],
                ret.at[slots(x), :],
                b_send.at[d],
                b_recv.at[d],
                {"ctx": ctx, "exp": e},
            )
        )
    for cp in back:
        cp.start()
    ret[slots(x), :] = comb[:, cols_of(x)]
    for k in range(4):
        for d in (0, 1):
            sum_copy(d, k, 1).wait_send()
    for cp in back:
        cp.wait()
    out_ref[...] = jnp.dot(coll_ref[...], ret[...], preferred_element_type=F32).astype(BF16)


def on_device(
    nz,
    nx,
    queries,
    new_keys,
    new_values,
    cache_keys,
    cache_values,
    offset,
    token_ids,
    expert_table,
    norm_gain,
    w_gate,
    w_up,
    w_down,
):
    T = queries.shape[0]
    cap = T // 2
    width = norm_gain.shape[0]
    QW = queries.shape[1] // 2
    span = cache_keys.shape[0] + new_keys.shape[0]
    ff = w_gate.shape[2]
    chosen = expert_table.at[token_ids].get(mode="promise_in_bounds")
    index = jnp.arange(T, dtype=jnp.int32)
    same = (chosen[:, None] == chosen[None, :]) & (index[None, :] < index[:, None])
    slot = jnp.sum(same.astype(jnp.int32), axis=1)
    target = chosen * cap + slot
    places = jnp.arange(nx * cap, dtype=jnp.int32)
    dispatch = (places[:, None] == target[None, :]).astype(BF16)
    dispatch = jnp.pad(dispatch, ((0, 0), (0, HEAD - T))) if T < HEAD else dispatch
    collect = (target[:, None] == places[None, :]).astype(BF16)
    half = nz // 2
    lanes = 2 * T * (QW // HEAD)
    hbm = pl.BlockSpec(memory_space=pltpu.HBM)
    vmem = pl.BlockSpec(memory_space=pltpu.VMEM)
    dma = pltpu.SemaphoreType.DMA
    return pl.pallas_call(
        functools.partial(layer_kernel, nz, nx),
        out_shape=jax.ShapeDtypeStruct(queries.shape, BF16),
        in_specs=[pl.BlockSpec(memory_space=pltpu.SMEM)] + [hbm] * 6 + [vmem] * 2 + [hbm] * 3,
        out_specs=vmem,
        scratch_shapes=[
            pltpu.VMEM((nz, 2, span, HEAD), BF16),
            pltpu.VMEM((nz, 2, span, HEAD), BF16),
            pltpu.VMEM((2, T, QW), BF16),
            pltpu.VMEM((lanes, HEAD), BF16),
            pltpu.VMEM((2,) + dispatch.shape, BF16),
            pltpu.VMEM((1, lanes), jnp.int32),
            pltpu.VMEM((1, lanes), F32),
            pltpu.VMEM((1, lanes), F32),
            pltpu.VMEM((HEAD, lanes), F32),
            pltpu.VMEM((2 * T, QW), BF16),
            pltpu.VMEM((2, nx * cap, QW), BF16),
            pltpu.VMEM((cap, width), BF16),
            pltpu.VMEM((nz * cap, width), BF16),
            pltpu.VMEM((nz * cap, width), BF16),
            pltpu.VMEM((2, half * cap, width), BF16),
            pltpu.VMEM((4 * cap, ff), F32),
            pltpu.VMEM((2, 4 * cap, ff), BF16),
            pltpu.VMEM((cap, width), BF16),
            pltpu.VMEM((nx * cap, width // nx), BF16),
            pltpu.VMEM((2,) + w_gate.shape[1:], BF16),
            pltpu.VMEM((2,) + w_up.shape[1:], BF16),
            pltpu.VMEM((2,) + w_down.shape[1:], BF16),
            dma((6,)),
            dma((6,)),
            dma((6,)),
            dma((3,)),
            dma((3,)),
            dma((3,)),
            dma((2, 4)),
            dma((2, half, 4)),
            dma((nx, 2)),
            dma((nx, 2)),
            dma((2, 4)),
            dma((2, half, 4)),
            dma((2, 4)),
            dma((2, half, 4)),
            dma((nx,)),
            dma((nx,)),
        ],
        compiler_params=pltpu.CompilerParams(
            collective_id=0, has_side_effects=True, vmem_limit_bytes=VMEM_LIMIT
        ),
    )(
        offset,
        queries,
        new_keys,
        new_values,
        cache_keys,
        cache_values,
        dispatch,
        collect,
        norm_gain.reshape(1, width),
        w_gate,
        w_up,
        w_down,
    )


def solution(mesh):
    split = ("group", "ctx")
    tokens = P(split, "exp")
    placed = (
        tokens,
        tokens,
        tokens,
        tokens,
        tokens,
        P("group"),
        P(split),
        P("group"),
        P(),
        P("exp", None, "ctx"),
        P("exp", None, "ctx"),
        P("exp", "ctx", None),
    )
    return jax.shard_map(
        functools.partial(on_device, mesh.shape["ctx"] // 2, mesh.shape["exp"]),
        mesh=mesh,
        in_specs=placed,
        out_specs=tokens,
        check_vma=False,
    )
```

time: 401 us -> 207 us (0.52)
  waiting for transfers between devices: 266 us -> 0 us
  Pallas kernels: 0 us -> 189 us
  matrix products: 46.4 us -> 0 us
  blocking collectives: 22.3 us -> 0 us
  local copies, waits for them, and re-layouts: 36.1 us -> 15.2 us
  between operations: 13.9 us -> 0.73 us
  other arithmetic: 15.2 us -> 2.18 us
    pallas_call x0 -> x1, Pallas kernels: none -> 189 us  [on_device(): pl.pallas_call(functools.partial(layer_kernel, nz, nx), out_shape=jax.Sha...]
    all_gather x2 -> x0, waiting for transfers between devices: 161 us -> none  [the longest x1 89.4 us: sent_together(): filled = lax.all_gather(both, axis, axis=dim, tiled=True)]
    reduce_scatter x2 -> x0, waiting for transfers between devices: 105 us -> none  [own_block(): tiles = lax.psum_scatter(tiles, axes[k], scatter_dimension=0, tiled=True)]
    dot_general x6 -> x0, matrix products: 46.4 us -> none  [the longest x1 15.2 us: on_device(): jnp.dot(hidden, down_w, preferred_element_type=jnp.float32)]
    all_to_all x2 -> x0, blocking collectives: 22.3 us -> none  [the longest x1 11.2 us: on_device(): lax.all_to_all(combined, 'exp', split_axis=1, concat_axis=0, tiled=True)]
    reduce_sum x3 -> x1, other arithmetic: 10.6 us -> 0.18 us  [on_device(): slot = jnp.sum(same.astype(jnp.int32), axis=1)]
    split x1 -> x0, local copies, waits for them, and re-layouts: 8.86 us -> none  [sent_together(): jnp.split(filled, [sum(widths[:k]) for k in range(1, len(widths))], axis=...]
    another operation x1 -> x0, local copies, waits for them, and re-layouts: 7.71 us -> none  [own_block(): tiles = tiles.reshape(*shape, *tiles.shape[1:])]
  transfers between devices with their start and end apart: 4 -> 0, of which waited for: 4 -> 0; matrix products, arithmetic and copies ran while one was open for 1% -> 0% of each run, Pallas kernels for 0% -> 0%
where the time goes in v1:
time: 207 us
  Pallas kernels  189 us (91%)
  local copies, waits for them, and re-layouts  15.2 us (7%)
  other arithmetic  2.18 us (1%)
    pallas_call x1, Pallas kernels, on_device(): pl.pallas_call(functools.partial(layer_kernel, nz, nx), out_shape=jax.Sha...  189 us
    unnamed x5, local copies, waits for them, and re-layouts  14.5 us

profile of v1, /device:TPU:40, one launch (start us, length us, event | category | flops | bytes accessed | tf_op | source)
XLA Modules:
  0.0 206.9 jit_solution(17383049347741753741)
XLA Ops:
  0.0 0.0 copy-start
  0.7 0.7 compare_select_fusion
  1.4 0.0 copy-done
  1.4 0.8 gather_fusion
  2.2 0.2 convert_reduce_fusion
  2.3 0.7 fusion.1.coll_ref
  3.0 0.6 pad_convert_fusion.disp_hbm
  3.7 6.4 %copy.17.wg_hbm = bf16[1,4096,448]{2,1,0:T(8,128)(2,1)} copy(bf16[1,4096,448]{1,2,0:T(8,128)(2,1)} %param.21) | data formatting | bytes 7340032 | tf_op args[9]
  10.1 6.5 %copy.18.wu_hbm = bf16[1,4096,448]{2,1,0:T(8,128)(2,1)} copy(bf16[1,4096,448]{1,2,0:T(8,128)(2,1)} %param.22) | data formatting | bytes 7340032 | tf_op args[10]
  16.6 188.8 %shard_map.118 = bf16[64,1024]{1,0:T(8,128)(2,1)} custom-call(s32[1]{0:T(128)S(6)} %copy.20.offset_ref, bf16[64,1024]{1,0:T(8,128)(2,1)} %q_hbm.1, bf16[64,256]{1,0:T(8,128)(2,1)} %nk_hbm.1, bf16[64,256]{1,0:T(8,128)(2,1)} %nv_hbm.1, bf16[256,256]{1,0:T(8,128)(2,1)} %ck_hbm.1, bf16[256,256]{1,0:T(8,128)(2,1)} %cv_hbm.1, ...), custom_call_target="tpu_custom_call" | custom-call | tf_op jit(solution)/shard_map/pallas_call | solution.py:505
  205.3 1.6 copy.21
  (3 shorter events, 0.0 us)
Async XLA Ops:
  0.0 1.4 copy-start

commit v2 on v1

v2 whole, which is shorter than its diff:
```python
import functools
import math

import jax
import jax.numpy as jnp
from jax import lax
from jax.experimental import pallas as pl
from jax.experimental.pallas import tpu as pltpu
from jax.sharding import PartitionSpec as P

MESH = pl.DeviceIdType.MESH
F32 = jnp.float32
BF16 = jnp.bfloat16
HEAD = 128
NEG = -1e30
VMEM_LIMIT = 64000 * 1024
LAG = 2


def layer_kernel(
    nz,
    nx,
    offset_ref,
    ids_ref,
    q_hbm,
    nk_hbm,
    nv_hbm,
    ck_hbm,
    cv_hbm,
    table_hbm,
    gain_ref,
    wg_hbm,
    wu_hbm,
    wd_hbm,
    out_ref,
    coll_ref,
    kbuf,
    vbuf,
    qbuf,
    qcat,
    cbuf,
    table,
    found,
    tok_ref,
    m_ref,
    l_ref,
    o_ref,
    att,
    packed,
    arr,
    rows,
    sums,
    rsb,
    gate_s,
    hid,
    comb,
    ret,
    wg,
    wu,
    wd,
    loc_sem,
    pair_send,
    pair_recv,
    w_loc,
    w_send,
    w_recv,
    kv_send,
    kv_recv,
    a_send,
    a_recv,
    g_send,
    g_recv,
    r_send,
    r_recv,
    b_send,
    b_recv,
):
    ctx = lax.axis_index("ctx")
    x = lax.axis_index("exp")
    z = ctx // 2
    c = ctx % 2
    oc = 1 - c
    half = nz // 2
    right = {"ctx": ((z + 1) % nz) * 2 + c, "exp": x}
    left = {"ctx": ((z + nz - 1) % nz) * 2 + c, "exp": x}
    ahead = (right, left)
    pair = {"ctx": z * 2 + oc, "exp": x}
    T = q_hbm.shape[0]
    CK = ck_hbm.shape[0]
    NK = nk_hbm.shape[0]
    QW = qbuf.shape[2]
    group = QW // HEAD
    cap = arr.shape[0]
    width = arr.shape[1]
    hrow = cap // 2
    hcol = width // 2

    def remote(src, dst, ssem, rsem, dev):
        return pltpu.make_async_remote_copy(
            src_ref=src, dst_ref=dst, send_sem=ssem, recv_sem=rsem, device_id=dev, device_id_type=MESH
        )

    kcol = pl.ds(pl.multiple_of(c * HEAD, HEAD), HEAD)
    kcol_o = pl.ds(pl.multiple_of(oc * HEAD, HEAD), HEAD)
    qcol = pl.ds(pl.multiple_of(c * QW, HEAD), QW)
    qcol_o = pl.ds(pl.multiple_of(oc * QW, HEAD), QW)
    parts = (
        (ck_hbm, kbuf, 0, CK),
        (nk_hbm, kbuf, CK, NK),
        (cv_hbm, vbuf, 0, CK),
        (nv_hbm, vbuf, CK, NK),
    )
    local = []
    for i, (src, buf, lo, n) in enumerate(parts):
        local.append(
            pltpu.make_async_copy(src.at[:, kcol], buf.at[0, 0, pl.ds(lo, n), :], loc_sem.at[i])
        )
    local.append(pltpu.make_async_copy(q_hbm.at[:, qcol], qbuf.at[0], loc_sem.at[4]))
    local.append(pltpu.make_async_copy(table_hbm, table, loc_sem.at[5]))
    for cp in local:
        cp.start()

    barrier = pltpu.get_barrier_semaphore()
    others = []
    for d in range(nx):
        for k in range(2):
            if d or k:
                others.append((d, k))
    for dev in ahead:
        pl.semaphore_signal(barrier, inc=1, device_id=dev, device_id_type=MESH)
    for d, k in others:
        pl.semaphore_signal(
            barrier,
            inc=1,
            device_id={"ctx": z * 2 + (c + k) % 2, "exp": (x + d) % nx},
            device_id_type=MESH,
        )
    pl.semaphore_wait(barrier, 2 + len(others))

    swap = []
    for i, (src, buf, lo, n) in enumerate(parts):
        swap.append(
            remote(src.at[:, kcol_o], buf.at[0, 1, pl.ds(lo, n), :], pair_send.at[i], pair_recv.at[i], pair)
        )
    swap.append(remote(q_hbm.at[:, qcol_o], qbuf.at[1], pair_send.at[4], pair_recv.at[4], pair))
    for cp in swap:
        cp.start()

    def last_pos(d, s):
        return 2 * s - 1 if d == 0 else 2 * s - s // half

    def kv_chunk(k, pos):
        return (kbuf, vbuf)[k % 2].at[pos, k // 2]

    def kv_copy(d, k, s, pos):
        return remote(
            kv_chunk(k, pos),
            kv_chunk(k, last_pos(d, s)),
            kv_send.at[d, k],
            kv_recv.at[d, s - 1, k],
            ahead[d],
        )

    for i in range(4):
        local[i].wait()
    for k in (0, 1):
        for d in (0, 1):
            kv_copy(d, k, 1, 0).start()
    local[4].wait()
    for i in range(4):
        swap[i].wait_recv()
    for k in (2, 3):
        for d in (0, 1):
            kv_copy(d, k, 1, 0).start()

    weights = ((wg_hbm, wg), (wu_hbm, wu), (wd_hbm, wd))
    w_own = [pltpu.make_async_copy(src.at[0], dst.at[0], w_loc.at[i]) for i, (src, dst) in enumerate(weights)]
    w_swap = [remote(src.at[0], dst.at[1], w_send.at[i], w_recv.at[i], pair) for i, (src, dst) in enumerate(weights)]
    for cp in w_own:
        cp.start()
    for cp in w_swap:
        cp.start()

    swap[4].wait_recv()
    for g in range(group):
        for s in range(2):
            qcat[pl.ds((g * 2 + s) * T, T), :] = qbuf[s, :, pl.ds(g * HEAD, HEAD)]
    lanes = 2 * T * group
    lane = lax.broadcasted_iota(jnp.int32, (1, lanes), 1)
    bits = T.bit_length() - 1
    second = lax.shift_right_logical(lane, bits) & 1
    tok_ref[...] = z * (2 * T) + (lane & (T - 1)) + jnp.where(second == 0, c, oc) * T
    m_ref[...] = jnp.full_like(m_ref, NEG)
    l_ref[...] = jnp.zeros_like(l_ref)
    o_ref[...] = jnp.zeros_like(o_ref)
    scale = 1.0 / math.sqrt(HEAD)

    local[5].wait()
    one_row = lax.broadcasted_iota(jnp.int32, (1, HEAD), 1)

    def look_up(t, carry):
        name = ids_ref[t]
        line = table[pl.ds(lax.shift_right_logical(name, 7), 1), :]
        found[pl.ds(t, 1), :] = jnp.where(one_row == (name & 127), line, 0)
        return carry

    lax.fori_loop(0, T, look_up, 0)
    chosen = jnp.sum(found[...], axis=1, keepdims=True)
    places = lax.broadcasted_iota(jnp.int32, (T, cbuf.shape[2]), 1)
    onehot = (places == chosen).astype(F32)
    before = (
        lax.broadcasted_iota(jnp.int32, (T, T), 1) < lax.broadcasted_iota(jnp.int32, (T, T), 0)
    ).astype(F32)
    earlier = jnp.dot(before.astype(BF16), onehot.astype(BF16), preferred_element_type=F32)
    slot = jnp.sum(earlier * onehot, axis=1, keepdims=True)
    target = chosen * cap + slot.astype(jnp.int32)
    collect = (places == target).astype(F32).astype(BF16)
    cbuf[0] = collect
    coll_ref[...] = collect
    c_swap = remote(cbuf.at[0], cbuf.at[1], pair_send.at[5], pair_recv.at[5], pair)
    c_swap.start()
    nt = (((1,), (1,)), ((), ()))
    tn = (((0,), (0,)), ((), ()))

    def attend(pos, src, zz):
        owner = zz * 2 + (c if src == 0 else oc)
        s = lax.dot_general(kbuf[pos, src], qcat[...], nt, preferred_element_type=F32) * scale
        crow = lax.broadcasted_iota(jnp.int32, (CK, 1), 0) + owner * CK
        sc = jnp.where(crow < offset_ref[0], s[:CK], NEG)
        nrow = lax.broadcasted_iota(jnp.int32, (NK, lanes), 0) + owner * NK
        sn = jnp.where(nrow <= tok_ref[...], s[CK:], NEG)
        m_old = m_ref[...]
        m_new = jnp.maximum(
            m_old,
            jnp.maximum(jnp.max(sc, axis=0, keepdims=True), jnp.max(sn, axis=0, keepdims=True)),
        )
        pc = jnp.exp(sc - m_new)
        pn = jnp.exp(sn - m_new)
        fade = jnp.exp(m_old - m_new)
        m_ref[...] = m_new
        l_ref[...] = (
            l_ref[...] * fade + jnp.sum(pc, axis=0, keepdims=True) + jnp.sum(pn, axis=0, keepdims=True)
        )
        p = jnp.concatenate([pc.astype(BF16), pn.astype(BF16)], axis=0)
        o_ref[...] = o_ref[...] * fade + lax.dot_general(vbuf[pos, src], p, tn, preferred_element_type=F32)

    def kv_step(s, carry):
        for k in range(4):
            for d in (0, 1):
                here = last_pos(d, s)
                kv_copy(d, k, s, here).wait_recv()
                onward = kv_copy(d, k, s + 1, here)
                if k // 2 == d:
                    onward.wait_send()
                    onward.start()
                else:

                    @pl.when(s < half - 1)
                    def _():
                        onward.wait_send()
                        onward.start()

            if k < 2:

                @pl.when(s > 1)
                def _():
                    attend(2 * s - 3, k, (z + nz - s + 1) % nz)

            else:
                attend(2 * s - 2, k - 2, (z + s - 1) % nz)
        return carry

    lax.fori_loop(1, half, kv_step, 0)
    for k in range(2):
        attend(2 * half - 3, k, (z + nz - half + 1) % nz)
    for k in range(2):
        attend(2 * half - 2, k, (z + half - 1) % nz)
    for d in (0, 1):
        for k in (2 * d, 2 * d + 1):
            kv_copy(d, k, half, 2 * half - 1).wait_recv()
        attend(2 * half - 1, d, (z + half) % nz)
    for k in range(4):
        for d in (0, 1):
            kv_copy(d, k, half, 0).wait_send()
    for cp in swap:
        cp.wait_send()

    done = o_ref[...] / l_ref[...]
    for g in range(group):
        att[:, pl.ds(g * HEAD, HEAD)] = done[:, g * 2 * T : (g + 1) * 2 * T].T.astype(BF16)
    c_swap.wait()
    for k in range(2):
        packed[k] = lax.dot_general(
            cbuf[k], att[pl.ds(k * T, T), :], tn, preferred_element_type=F32
        ).astype(BF16)

    mine = pl.ds(pl.multiple_of((x * 2 + c) * QW, HEAD), QW)

    def slots(e, h):
        return pl.ds(pl.multiple_of(e * cap + h * hrow, hrow), hrow)

    def row_half(h):
        return pl.ds(h * hrow, hrow)

    there = ([], [])
    for h in range(2):
        for d, k in others:
            e = (x + d) % nx
            there[h].append(
                remote(
                    packed.at[k, slots(e, h), :],
                    arr.at[row_half(h), mine],
                    a_send.at[h, d, k],
                    a_recv.at[h, d, k],
                    {"ctx": z * 2 + (c + k) % 2, "exp": e},
                )
            )
        for cp in there[h]:
            cp.start()
        arr[row_half(h), mine] = packed[0, slots(x, h), :]

    lot = nz * hrow

    def part(ref, h, pos, q):
        return ref.at[pl.ds(pl.multiple_of(h * lot + pos * hrow, hrow), hrow), pl.ds(q * hcol, hcol)]

    def normalize(h):
        for cp in there[h]:
            cp.wait_recv()
        v32 = arr[row_half(h), :].astype(F32)
        norm = lax.rsqrt(jnp.mean(v32 * v32, axis=-1, keepdims=True) + 1e-05)
        rows[pl.ds(h * lot, hrow), :] = (v32 * norm * gain_ref[...]).astype(BF16)

    def row_copy(h, q, d, s, pos):
        return remote(
            part(rows, h, pos, q),
            part(rows, h, last_pos(d, s), q),
            g_send.at[d, h * 2 + q],
            g_recv.at[d, s - 1, h * 2 + q],
            ahead[d],
        )

    normalize(0)
    for q in range(2):
        for d in (0, 1):
            row_copy(0, q, d, 1, 0).start()
    normalize(1)
    for cp in w_own:
        cp.wait()
    for cp in w_swap:
        cp.wait()

    M = lot // 2
    ncol = width // 4

    def dense(w, i):
        lo = pl.multiple_of((w % 2) * lot + (w // 2) * M, M)
        if i < 4:
            src = i // 2
            mat = (wg, wu)[i % 2]
            v = lax.dot_general(mat[src], rows[pl.ds(lo, M), :], nt, preferred_element_type=F32)
            if i % 2 == 0:
                gate_s[...] = v
            else:
                g32 = gate_s[...]
                hid[src] = (g32 / (1.0 + jnp.exp(-g32)) * v).T.astype(BF16)
        else:
            cols = pl.ds((i - 4) * ncol, ncol)
            sums[pl.ds(lo, M), cols] = (
                jnp.dot(hid[0], wd[0, :, cols], preferred_element_type=F32)
                + jnp.dot(hid[1], wd[1, :, cols], preferred_element_type=F32)
            ).astype(BF16)

    first_turn = half // 4
    last_turn = (half + LAG) // 2

    def row_pair(j, carry):
        for o in range(2):
            t = 2 * j + 1 + o
            for h in range(2):
                s = t - LAG * h
                for q in range(2):
                    for d in (0, 1):

                        def take(keep=q == d, h=h, q=q, d=d, s=s):
                            here = last_pos(d, s)
                            arrive = row_copy(h, q, d, s, here)
                            onward = row_copy(h, q, d, s + 1, here)

                            def on():
                                onward.wait_send()
                                onward.start()

                            if keep:
                                arrive.wait_recv()
                                pl.when(s < half)(on)
                            else:

                                @pl.when(s < half)
                                def _():
                                    arrive.wait_recv()
                                    pl.when(s < half - 1)(on)

                        if h == 0:
                            pl.when(s <= half)(take)
                        else:
                            pl.when(s > 0)(take)

                            @pl.when(s == 0)
                            def _():
                                row_copy(h, q, d, 1, 0).start()

                    @pl.when(j >= first_turn)
                    def _():
                        dense(j - first_turn, o * 4 + h * 2 + q)

        return carry

    lax.fori_loop(0, last_turn, row_pair, 0)
    for w in range(last_turn - first_turn, 3):
        for i in range(8):
            dense(w, i)
    for cp in there[0] + there[1]:
        cp.wait_send()
    for h in range(2):
        for q in range(2):
            for d in (0, 1):
                row_copy(h, q, d, half, 0).wait_send()

    def sum_copy(h, q, d, s):
        pos = 2 * s - s // half if d == 0 else 2 * s - 1
        return remote(
            part(sums, h, pos, q),
            rsb.at[d, s - 1, row_half(h), pl.ds(q * hcol, hcol)],
            r_send.at[d, h * 2 + q],
            r_recv.at[d, s - 1, h * 2 + q],
            ahead[d],
        )

    def sum_first(h, q, d, s):
        sum_copy(h, q, d, s).start()

    def sum_next(h, q, d, s):
        pos = 2 * s if d == 0 else 2 * s - 1
        sum_copy(h, q, d, s + 1).wait_recv()
        own = part(sums, h, pos, q)
        came = rsb[d, s, row_half(h), pl.ds(q * hcol, hcol)]
        own[...] = (own[...].astype(F32) + came.astype(F32)).astype(BF16)
        sum_copy(h, q, d, s).wait_send()
        sum_copy(h, q, d, s).start()

    def sum_start(h):
        for d in (0, 1):
            sum_first(h, d, d, half)
        for d in (0, 1):
            sum_first(h, 1 - d, d, half - 1)

    def sum_keep(h):
        for d in (0, 1):
            sum_next(h, d, d, half - 1)

    def sum_step(h, s):
        for r in (1, 0):
            for d in (0, 1):
                sum_next(h, d if r == 0 else 1 - d, d, s)

    tw = width // nx

    def cols_of(e):
        return pl.ds(pl.multiple_of(e * tw, HEAD), tw)

    def finish(h):
        for q in range(2):
            for d in (0, 1):
                sum_copy(h, q, d, 1).wait_recv()
            cols = pl.ds(q * hcol, hcol)
            total = part(rows, h, 0, q)[...].astype(F32) + (
                part(sums, h, 0, q)[...].astype(F32)
                + rsb[0, 0, row_half(h), cols].astype(F32)
                + rsb[1, 0, row_half(h), cols].astype(F32)
            )
            comb[row_half(h), cols] = total.astype(BF16)
        back = []
        for d in range(1, nx):
            e = (x + d) % nx
            back.append(
                remote(
                    comb.at[row_half(h), cols_of(e)],
                    ret.at[slots(x, h), :],
                    b_send.at[h, d],
                    b_recv.at[h, d],
                    {"ctx": ctx, "exp": e},
                )
            )
        for cp in back:
            cp.start()
        ret[slots(x, h), :] = comb[row_half(h), cols_of(x)]
        return back

    sum_start(0)
    for i in range(4):
        dense(3, i)
    sum_keep(0)
    for i in range(4, 8):
        dense(3, i)
    sum_step(0, half - 2)
    sum_start(1)
    sum_step(0, half - 3)
    sum_keep(1)

    def sum_both(t, carry):
        sum_step(0, half - 4 - t)
        sum_step(1, half - 2 - t)
        return carry

    lax.fori_loop(0, half - 4, sum_both, 0)
    back = finish(0)
    sum_step(1, 2)
    sum_step(1, 1)
    back = back + finish(1)
    for h in range(2):
        for q in range(2):
            for d in (0, 1):
                sum_copy(h, q, d, 1).wait_send()
    for cp in back:
        cp.wait()
    out_ref[...] = ret[...]


def on_device(
    nz,
    nx,
    queries,
    new_keys,
    new_values,
    cache_keys,
    cache_values,
    offset,
    token_ids,
    expert_table,
    norm_gain,
    w_gate,
    w_up,
    w_down,
):
    T = queries.shape[0]
    cap = T // 2
    width = norm_gain.shape[0]
    QW = queries.shape[1] // 2
    span = cache_keys.shape[0] + new_keys.shape[0]
    ff = w_gate.shape[2]
    half = nz // 2
    lanes = 2 * T * (QW // HEAD)
    hbm = pl.BlockSpec(memory_space=pltpu.HBM)
    vmem = pl.BlockSpec(memory_space=pltpu.VMEM)
    smem = pl.BlockSpec(memory_space=pltpu.SMEM)
    dma = pltpu.SemaphoreType.DMA
    returned, collect = pl.pallas_call(
        functools.partial(layer_kernel, nz, nx),
        out_shape=(
            jax.ShapeDtypeStruct((nx * cap, width // nx), BF16),
            jax.ShapeDtypeStruct((T, nx * cap), BF16),
        ),
        in_specs=[smem] * 2 + [hbm] * 6 + [vmem] + [hbm] * 3,
        out_specs=(vmem, vmem),
        scratch_shapes=[
            pltpu.VMEM((nz, 2, span, HEAD), BF16),
            pltpu.VMEM((nz, 2, span, HEAD), BF16),
            pltpu.VMEM((2, T, QW), BF16),
            pltpu.VMEM((lanes, HEAD), BF16),
            pltpu.VMEM((2, T, nx * cap), BF16),
            pltpu.VMEM((expert_table.shape[0] // HEAD, HEAD), jnp.int32),
            pltpu.VMEM((T, HEAD), jnp.int32),
            pltpu.VMEM((1, lanes), jnp.int32),
            pltpu.VMEM((1, lanes), F32),
            pltpu.VMEM((1, lanes), F32),
            pltpu.VMEM((HEAD, lanes), F32),
            pltpu.VMEM((2 * T, QW), BF16),
            pltpu.VMEM((2, nx * cap, QW), BF16),
            pltpu.VMEM((cap, width), BF16),
            pltpu.VMEM((nz * cap, width), BF16),
            pltpu.VMEM((nz * cap, width), BF16),
            pltpu.VMEM((2, half, cap, width), BF16),
            pltpu.VMEM((ff, nz * cap // 4), F32),
            pltpu.VMEM((2, nz * cap // 4, ff), BF16),
            pltpu.VMEM((cap, width), BF16),
            pltpu.VMEM((nx * cap, width // nx), BF16),
            pltpu.VMEM((2, ff, width), BF16),
            pltpu.VMEM((2, ff, width), BF16),
            pltpu.VMEM((2,) + w_down.shape[1:], BF16),
            dma((6,)),
            dma((6,)),
            dma((6,)),
            dma((3,)),
            dma((3,)),
            dma((3,)),
            dma((2, 4)),
            dma((2, half, 4)),
            dma((2, nx, 2)),
            dma((2, nx, 2)),
            dma((2, 4)),
            dma((2, half, 4)),
            dma((2, 4)),
            dma((2, half, 4)),
            dma((2, nx)),
            dma((2, nx)),
        ],
        compiler_params=pltpu.CompilerParams(
            collective_id=0, has_side_effects=True, vmem_limit_bytes=VMEM_LIMIT
        ),
    )(
        offset,
        token_ids,
        queries,
        new_keys,
        new_values,
        cache_keys,
        cache_values,
        expert_table.reshape(-1, HEAD),
        norm_gain.reshape(1, width),
        jnp.swapaxes(w_gate, 1, 2),
        jnp.swapaxes(w_up, 1, 2),
        w_down,
    )
    return jnp.dot(collect, returned, preferred_element_type=F32).astype(BF16)


def solution(mesh):
    split = ("group", "ctx")
    tokens = P(split, "exp")
    placed = (
        tokens,
        tokens,
        tokens,
        tokens,
        tokens,
        P("group"),
        P(split),
        P("group"),
        P(),
        P("exp", None, "ctx"),
        P("exp", None, "ctx"),
        P("exp", "ctx", None),
    )
    return jax.shard_map(
        functools.partial(on_device, mesh.shape["ctx"] // 2, mesh.shape["exp"]),
        mesh=mesh,
        in_specs=placed,
        out_specs=tokens,
        check_vma=False,
    )
```

time: 207 us -> 196 us (0.947)
  local copies, waits for them, and re-layouts: 15.2 us -> 0 us
  Pallas kernels: 189 us -> 194 us
  other arithmetic: 2.18 us -> 0 us
    unnamed x5 -> x0, local copies, waits for them, and re-layouts: 14.5 us -> none
    pallas_call x1, Pallas kernels: 189 us -> 194 us  [on_device(): pl.pallas_call(functools.partial(layer_kernel, nz, nx), out_shape=(jax.Sh...]
where the time goes in v2:
time: 196 us
  Pallas kernels  194 us (99%)
    pallas_call x1, Pallas kernels, on_device(): pl.pallas_call(functools.partial(layer_kernel, nz, nx), out_shape=(jax.Sh...  194 us

profile of v2, /device:TPU:40, one launch (start us, length us, event | category | flops | bytes accessed | tf_op | source)
XLA Modules:
  0.0 196.1 jit_solution(3205454667204345824)
XLA Ops:
  0.7 193.6 %shard_map.118 = (bf16[128,1024]{1,0:T(8,128)(2,1)}, bf16[64,128]{1,0:T(8,128)(2,1)}) custom-call(s32[1]{0:T(128)S(6)} %copy.13.offset_ref, s32[64]{0:T(128)} %ids_ref.1, bf16[64,1024]{1,0:T(8,128)(2,1)} %q_hbm.1, bf16[64,256]{1,0:T(8,128)(2,1)} %nk_hbm.1, bf16[64,256]{1,0:T(8,128)(2,1)} %nv_hbm.1, bf16[256,256]{1,0:T(8,128)(2,1)} %ck_hbm.1, ...), custom_call_target="tpu_custom_call" | custom-call | tf_op jit(solution)/shard_map/pallas_call | solution.py:558
  194.3 1.8 convolution_convert_fusion

commit v3 on v1

--- a/solution.py
+++ b/solution.py
@@ -20,13 +20,13 @@
     nz,
     nx,
     offset_ref,
+    ids_ref,
     q_hbm,
     nk_hbm,
     nv_hbm,
     ck_hbm,
     cv_hbm,
-    disp_hbm,
-    coll_ref,
+    table_hbm,
     gain_ref,
     wg_hbm,
     wu_hbm,
@@ -36,7 +36,9 @@
     vbuf,
     qbuf,
     qcat,
-    dbuf,
+    cbuf,
+    table,
+    found,
     tok_ref,
     m_ref,
     l_ref,
@@ -47,7 +49,7 @@
     rows,
     sums,
     rsb,
-    gate_s,
+    acc,
     hid,
     comb,
     ret,
@@ -112,7 +114,7 @@
             pltpu.make_async_copy(src.at[:, kcol], buf.at[0, 0, pl.ds(lo, n), :], loc_sem.at[i])
         )
     local.append(pltpu.make_async_copy(q_hbm.at[:, qcol], qbuf.at[0], loc_sem.at[4]))
-    local.append(pltpu.make_async_copy(disp_hbm, dbuf.at[0], loc_sem.at[5]))
+    local.append(pltpu.make_async_copy(table_hbm, table, loc_sem.at[5]))
     for cp in local:
         cp.start()
 
@@ -139,7 +141,6 @@
             remote(src.at[:, kcol_o], buf.at[0, 1, pl.ds(lo, n), :], pair_send.at[i], pair_recv.at[i], pair)
         )
     swap.append(remote(q_hbm.at[:, qcol_o], qbuf.at[1], pair_send.at[4], pair_recv.at[4], pair))
-    swap.append(remote(disp_hbm, dbuf.at[1], pair_send.at[5], pair_recv.at[5], pair))
     for cp in swap:
         cp.start()
 
@@ -164,7 +165,6 @@
         for d in (0, 1):
             kv_copy(d, k, 1, 0).start()
     local[4].wait()
-    local[5].wait()
     for i in range(4):
         swap[i].wait_recv()
     for k in (2, 3):
@@ -180,7 +180,6 @@
         cp.start()
 
     swap[4].wait_recv()
-    swap[5].wait_recv()
     for g in range(group):
         for s in range(2):
             qcat[pl.ds((g * 2 + s) * T, T), :] = qbuf[s, :, pl.ds(g * HEAD, HEAD)]
@@ -193,6 +192,29 @@
     l_ref[...] = jnp.zeros_like(l_ref)
     o_ref[...] = jnp.zeros_like(o_ref)
     scale = 1.0 / math.sqrt(HEAD)
+    local[5].wait()
+    one_row = lax.broadcasted_iota(jnp.int32, (1, HEAD), 1)
+
+    def look_up(t, carry):
+        name = ids_ref[t]
+        line = table[pl.ds(lax.shift_right_logical(name, 7), 1), :]
+        found[pl.ds(t, 1), :] = jnp.where(one_row == (name & 127), line, 0)
+        return carry
+
+    lax.fori_loop(0, T, look_up, 0)
+    chosen = jnp.sum(found[...], axis=1, keepdims=True)
+    places = lax.broadcasted_iota(jnp.int32, (T, cbuf.shape[2]), 1)
+    onehot = (places == chosen).astype(F32)
+    before = (
+        lax.broadcasted_iota(jnp.int32, (T, T), 1) < lax.broadcasted_iota(jnp.int32, (T, T), 0)
+    ).astype(F32)
+    earlier = jnp.dot(before.astype(BF16), onehot.astype(BF16), preferred_element_type=F32)
+    slot = jnp.sum(earlier * onehot, axis=1, keepdims=True)
+    target = chosen * cap + slot.astype(jnp.int32)
+    collect = (places == target).astype(F32).astype(BF16)
+    cbuf[0] = collect
+    c_swap = remote(cbuf.at[0], cbuf.at[1], pair_send.at[5], pair_recv.at[5], pair)
+    c_swap.start()
     nt = (((1,), (1,)), ((), ()))
     tn = (((0,), (0,)), ((), ()))
 
@@ -200,7 +222,7 @@
         owner = zz * 2 + (c if src == 0 else oc)
         s = lax.dot_general(kbuf[pos, src], qcat[...], nt, preferred_element_type=F32) * scale
         crow = lax.broadcasted_iota(jnp.int32, (CK, 1), 0) + owner * CK
-        sc = jnp.where(crow < offset_ref[0], s[:CK], NEG)
+        sc = jnp.where(crow < offset_ref[...], s[:CK], NEG)
         nrow = lax.broadcasted_iota(jnp.int32, (NK, lanes), 0) + owner * NK
         sn = jnp.where(nrow <= tok_ref[...], s[CK:], NEG)
         m_old = m_ref[...]
@@ -218,9 +240,13 @@
         p = jnp.concatenate([pc.astype(BF16), pn.astype(BF16)], axis=0)
         o_ref[...] = o_ref[...] * fade + lax.dot_general(vbuf[pos, src], p, tn, preferred_element_type=F32)
 
+    def turned(k, d):
+        return (k + 2 * d) % 4
+
     def kv_step(s, carry):
-        for k in range(4):
+        for i in range(4):
             for d in (0, 1):
+                k = turned(i, d)
                 here = last_pos(d, s)
                 kv_copy(d, k, s, here).wait_recv()
                 onward = kv_copy(d, k, s + 1, here)
@@ -234,14 +260,14 @@
                         onward.wait_send()
                         onward.start()
 
-            if k < 2:
+            if i < 2:
 
                 @pl.when(s > 1)
                 def _():
-                    attend(2 * s - 3, k, (z + nz - s + 1) % nz)
+                    attend(2 * s - 3, i, (z + nz - s + 1) % nz)
 
             else:
-                attend(2 * s - 2, k - 2, (z + s - 1) % nz)
+                attend(2 * s - 2, i - 2, (z + s - 1) % nz)
         return carry
 
     lax.fori_loop(1, half, kv_step, 0)
@@ -262,36 +288,43 @@
     done = o_ref[...] / l_ref[...]
     for g in range(group):
         att[:, pl.ds(g * HEAD, HEAD)] = done[:, g * 2 * T : (g + 1) * 2 * T].T.astype(BF16)
+    c_swap.wait()
     for k in range(2):
-        packed[k] = jnp.dot(
-            dbuf[k, :, pl.ds(0, T)], att[pl.ds(k * T, T), :], preferred_element_type=F32
+        packed[k] = lax.dot_general(
+            cbuf[k], att[pl.ds(k * T, T), :], tn, preferred_element_type=F32
         ).astype(BF16)
 
     mine = pl.ds(pl.multiple_of((x * 2 + c) * QW, HEAD), QW)
 
-    def slots(e):
-        return pl.ds(pl.multiple_of(e * cap, cap), cap)
-
-    there = []
-    for d, k in others:
-        e = (x + d) % nx
-        there.append(
-            remote(
-                packed.at[k, slots(e), :],
-                arr.at[:, mine],
-                a_send.at[d, k],
-                a_recv.at[d, k],
-                {"ctx": z * 2 + (c + k) % 2, "exp": e},
+    def slots(e, h):
+        return pl.ds(pl.multiple_of(e * cap + h * hrow, hrow), hrow)
+
+    def row_half(h):
+        return pl.ds(h * hrow, hrow)
+
+    there = ([], [])
+    for h in range(2):
+        for d, k in others:
+            e = (x + d) % nx
+            there[h].append(
+                remote(
+                    packed.at[k, slots(e, h), :],
+                    arr.at[row_half(h), mine],
+                    a_send.at[h, d, k],
+                    a_recv.at[h, d, k],
+                    {"ctx": z * 2 + (c + k) % 2, "exp": e},
+                )
             )
-        )
-    for cp in there:
-        cp.start()
-    arr[:, mine] = packed[0, slots(x), :]
-    for cp in there:
-        cp.wait_recv()
-    v32 = arr[...].astype(F32)
-    norm = lax.rsqrt(jnp.mean(v32 * v32, axis=-1, keepdims=True) + 1e-05)
-    rows[pl.ds(0, cap), :] = (v32 * norm * gain_ref[...]).astype(BF16)
+        for cp in there[h]:
+            cp.start()
+        arr[row_half(h), mine] = packed[0, slots(x, h), :]
+
+    def normalize(h):
+        for cp in there[h]:
+            cp.wait_recv()
+        v32 = arr[row_half(h), :].astype(F32)
+        norm = lax.rsqrt(jnp.mean(v32 * v32, axis=-1, keepdims=True) + 1e-05)
+        rows[row_half(h), :] = (v32 * norm * gain_ref[...]).astype(BF16)
 
     def part(ref, pos, k):
         return ref.at[
@@ -307,11 +340,11 @@
             ahead[d],
         )
 
-    for k in range(4):
-        for d in (0, 1):
-            row_copy(d, k, 1, 0).start()
-    for cp in there:
-        cp.wait_send()
+    for h in range(2):
+        normalize(h)
+        for k in (2 * h, 2 * h + 1):
+            for d in (0, 1):
+                row_copy(d, k, 1, 0).start()
     for cp in w_own:
         cp.wait()
     for cp in w_swap:
@@ -321,56 +354,47 @@
     ncols = 4
     ncol = width // ncols
 
+    def activate(src):
+        g32 = acc[2 * src]
+        hid[src] = (g32 / (1.0 + jnp.exp(-g32)) * acc[2 * src + 1]).T.astype(BF16)
+
+    def project(g, i, cols):
+        return lax.dot_general(
+            (wg, wu)[i % 2][i // 2, :, cols],
+            rows[pl.ds(pl.multiple_of(g * M, M), M), cols],
+            nt,
+            preferred_element_type=F32,
+        )
+
     def dense(g, i):
-        lo = pl.multiple_of(g * M, M)
         if i < 4:
-            src = i // 2
-            w = (wg, wu)[i % 2]
-            v = jnp.dot(rows[pl.ds(lo, M), :], w[src], preferred_element_type=F32)
-            if i % 2 == 0:
-                gate_s[...] = v
-            else:
-                g32 = gate_s[...]
-                hid[src] = (g32 / (1.0 + jnp.exp(-g32)) * v).astype(BF16)
+            acc[i] = project(g, i, pl.ds(0, width))
+            if i % 2:
+                activate(i // 2)
         else:
             cols = pl.ds((i - 4) * ncol, ncol)
-            sums[pl.ds(lo, M), cols] = (
+            sums[pl.ds(pl.multiple_of(g * M, M), M), cols] = (
                 jnp.dot(hid[0], wd[0, :, cols], preferred_element_type=F32)
                 + jnp.dot(hid[1], wd[1, :, cols], preferred_element_type=F32)
             ).astype(BF16)
 
     pairs = half // 2
 
+    def row_step(s, last):
+        for i in range(4):
+            for d in (0, 1):
+                k = turned(i, d)
+                here = last_pos(d, s)
+                row_copy(d, k, s, here).wait_recv()
+                if not last or k // 2 == d:
+                    onward = row_copy(d, k, s + 1, here)
+                    onward.wait_send()
+                    onward.start()
+            yield i
+
     def row_pair(j, carry):
-        more = j < pairs - 1
         for o in range(2):
-            s = 2 * j + 1 + o
-            for k in range(4):
-                for d in (0, 1):
-                    here = last_pos(d, s)
-                    arrive = row_copy(d, k, s, here)
-                    onward = row_copy(d, k, s + 1, here)
-                    keep = k // 2 == d
-
-                    def on():
-                        onward.wait_send()
-                        onward.start()
-
-                    if o == 0:
-                        arrive.wait_recv()
-                        if keep:
-                            on()
-                        else:
-                            pl.when(more)(on)
-                    elif keep:
-                        arrive.wait_recv()
-                        pl.when(more)(on)
-                    else:
-
-                        @pl.when(more)
-                        def _():
-                            arrive.wait_recv()
-                            on()
+            for k in row_step(2 * j + 1 + o, False):
 
                 @pl.when(j > 0)
                 def _():
@@ -378,10 +402,21 @@
 
         return carry
 
-    lax.fori_loop(0, pairs, row_pair, 0)
-    for k in range(4):
+    lax.fori_loop(0, pairs - 1, row_pair, 0)
+    tail = pairs - 1
+    for i in row_step(half - 1, True):
+        if i == 1 and tail > 0:
+            for piece in range(8):
+                dense(tail - 1, piece)
+    for q in range(2):
         for d in (0, 1):
-            row_copy(d, k, half, 0).wait_send()
+            row_copy(d, 2 * d + q, half, 2 * half - 1).wait_recv()
+        cols = pl.ds(q * hcol, hcol)
+        for i in range(4):
+            v = project(tail, i, cols)
+            acc[i] = v if q == 0 else acc[i] + v
+    for src in range(2):
+        activate(src)
 
     def sum_copy(d, k, s):
         pos = 2 * s - s // half if d == 0 else 2 * s - 1
@@ -393,9 +428,9 @@
             ahead[d],
         )
 
-    for i in range(8):
-        dense(pairs - 1, i)
     for q in range(2):
+        for i in (4 + 2 * q, 5 + 2 * q):
+            dense(tail, i)
         for d in (0, 1):
             sum_copy(d, 2 * d + q, half).start()
 
@@ -427,8 +462,36 @@
 
     lax.fori_loop(0, half - 1, sum_step, 0)
 
-    for h in range(2):
-        for q in range(2):
+    tw = width // nx
+    each = hcol // tw
+
+    def give_back(e, sends):
+        cols = pl.ds(e * tw, tw)
+        there_x = pl.ds(pl.multiple_of(x * cap, cap), cap)
+        step = (e - x + nx) % nx
+
+        @pl.when(e != x)
+        def _():
+            move = remote(
+                comb.at[:, cols],
+                ret.at[there_x, :],
+                b_send.at[step],
+                b_recv.at[step],
+                {"ctx": ctx, "exp": e},
+            )
+            if sends:
+                move.start()
+            else:
+                move.wait_send()
+
+        if sends:
+
+            @pl.when(e == x)
+            def _():
+                ret[there_x, :] = comb[:, cols]
+
+    for q in range(2):
+        for h in range(2):
             k = 2 * h + q
             for d in (0, 1):
                 sum_copy(d, k, 1).wait_recv()
@@ -438,32 +501,21 @@
                 + part(rsb.at[1], 0, k)[...].astype(F32)
             )
             part(comb, 0, k)[...] = total.astype(BF16)
-    tw = width // nx
-
-    def cols_of(e):
-        return pl.ds(pl.multiple_of(e * tw, HEAD), tw)
-
-    back = []
-    for d in range(1, nx):
-        e = (x + d) % nx
-        back.append(
-            remote(
-                comb.at[:, cols_of(e)],
-                ret.at[slots(x), :],
-                b_send.at[d],
-                b_recv.at[d],
-                {"ctx": ctx, "exp": e},
-            )
-        )
-    for cp in back:
-        cp.start()
-    ret[slots(x), :] = comb[:, cols_of(x)]
+        for e in range(q * each, (q + 1) * each):
+            give_back(e, True)
+    for cp in there[0] + there[1]:
+        cp.wait_send()
     for k in range(4):
         for d in (0, 1):
+            row_copy(d, k, half, 0).wait_send()
             sum_copy(d, k, 1).wait_send()
-    for cp in back:
-        cp.wait()
-    out_ref[...] = jnp.dot(coll_ref[...], ret[...], preferred_element_type=F32).astype(BF16)
+    for e in range(nx):
+        give_back(e, False)
+    for d in range(1, nx):
+        e = (x + nx - d) % nx
+        spot = pl.ds(pl.multiple_of(e * cap, cap), cap)
+        remote(comb.at[:, pl.ds(0, tw)], ret.at[spot, :], b_send.at[d], b_recv.at[d], {"ctx": ctx, "exp": e}).wait_recv()
+    out_ref[...] = jnp.dot(cbuf[0], ret[...], preferred_element_type=F32).astype(BF16)
 
 
 def on_device(
@@ -488,31 +540,25 @@
     QW = queries.shape[1] // 2
     span = cache_keys.shape[0] + new_keys.shape[0]
     ff = w_gate.shape[2]
-    chosen = expert_table.at[token_ids].get(mode="promise_in_bounds")
-    index = jnp.arange(T, dtype=jnp.int32)
-    same = (chosen[:, None] == chosen[None, :]) & (index[None, :] < index[:, None])
-    slot = jnp.sum(same.astype(jnp.int32), axis=1)
-    target = chosen * cap + slot
-    places = jnp.arange(nx * cap, dtype=jnp.int32)
-    dispatch = (places[:, None] == target[None, :]).astype(BF16)
-    dispatch = jnp.pad(dispatch, ((0, 0), (0, HEAD - T))) if T < HEAD else dispatch
-    collect = (target[:, None] == places[None, :]).astype(BF16)
     half = nz // 2
     lanes = 2 * T * (QW // HEAD)
     hbm = pl.BlockSpec(memory_space=pltpu.HBM)
     vmem = pl.BlockSpec(memory_space=pltpu.VMEM)
+    smem = pl.BlockSpec(memory_space=pltpu.SMEM)
     dma = pltpu.SemaphoreType.DMA
     return pl.pallas_call(
         functools.partial(layer_kernel, nz, nx),
         out_shape=jax.ShapeDtypeStruct(queries.shape, BF16),
-        in_specs=[pl.BlockSpec(memory_space=pltpu.SMEM)] + [hbm] * 6 + [vmem] * 2 + [hbm] * 3,
+        in_specs=[vmem, smem] + [hbm] * 6 + [vmem] + [hbm] * 3,
         out_specs=vmem,
         scratch_shapes=[
             pltpu.VMEM((nz, 2, span, HEAD), BF16),
             pltpu.VMEM((nz, 2, span, HEAD), BF16),
             pltpu.VMEM((2, T, QW), BF16),
             pltpu.VMEM((lanes, HEAD), BF16),
-            pltpu.VMEM((2,) + dispatch.shape, BF16),
+            pltpu.VMEM((2, T, nx * cap), BF16),
+            pltpu.VMEM((expert_table.shape[0] // HEAD, HEAD), jnp.int32),
+            pltpu.VMEM((T, HEAD), jnp.int32),
             pltpu.VMEM((1, lanes), jnp.int32),
             pltpu.VMEM((1, lanes), F32),
             pltpu.VMEM((1, lanes), F32),
@@ -523,12 +569,12 @@
             pltpu.VMEM((nz * cap, width), BF16),
             pltpu.VMEM((nz * cap, width), BF16),
             pltpu.VMEM((2, half * cap, width), BF16),
-            pltpu.VMEM((4 * cap, ff), F32),
+            pltpu.VMEM((4, ff, 4 * cap), F32),
             pltpu.VMEM((2, 4 * cap, ff), BF16),
             pltpu.VMEM((cap, width), BF16),
             pltpu.VMEM((nx * cap, width // nx), BF16),
-            pltpu.VMEM((2,) + w_gate.shape[1:], BF16),
-            pltpu.VMEM((2,) + w_up.shape[1:], BF16),
+            pltpu.VMEM((2, ff, width), BF16),
+            pltpu.VMEM((2, ff, width), BF16),
             pltpu.VMEM((2,) + w_down.shape[1:], BF16),
             dma((6,)),
             dma((6,)),
@@ -538,8 +584,8 @@
             dma((3,)),
             dma((2, 4)),
             dma((2, half, 4)),
-            dma((nx, 2)),
-            dma((nx, 2)),
+            dma((2, nx, 2)),
+            dma((2, nx, 2)),
             dma((2, 4)),
             dma((2, half, 4)),
             dma((2, 4)),
@@ -551,17 +597,17 @@
             collective_id=0, has_side_effects=True, vmem_limit_bytes=VMEM_LIMIT
         ),
     )(
-        offset,
+        offset.reshape(1, 1),
+        token_ids,
         queries,
         new_keys,
         new_values,
         cache_keys,
         cache_values,
-        dispatch,
-        collect,
+        expert_table.reshape(-1, HEAD),
         norm_gain.reshape(1, width),
-        w_gate,
-        w_up,
+        jnp.swapaxes(w_gate, 1, 2),
+        jnp.swapaxes(w_up, 1, 2),
         w_down,
     )
 

time: 207 us -> 189 us (0.913)
  local copies, waits for them, and re-layouts: 15.2 us -> 1.57 us
  other arithmetic: 2.18 us -> 0 us
    unnamed x5 -> x1, local copies, waits for them, and re-layouts: 14.5 us -> 1.57 us
where the time goes in v3:
time: 189 us
  Pallas kernels  187 us (99%)
    pallas_call x1, Pallas kernels, on_device(): pl.pallas_call(functools.partial(layer_kernel, nz, nx), out_shape=jax.Sha...  187 us

profile of v3, /device:TPU:40, one launch (start us, length us, event | category | flops | bytes accessed | tf_op | source)
XLA Modules:
  0.0 189.1 jit_solution(16000330172269736829)
XLA Ops:
  0.7 186.9 %shard_map.118 = bf16[64,1024]{1,0:T(8,128)(2,1)} custom-call(s32[1,1]{1,0:T(1,128)} %bitcast.5.offset_ref, s32[64]{0:T(128)} %ids_ref.1, bf16[64,1024]{1,0:T(8,128)(2,1)} %q_hbm.1, bf16[64,256]{1,0:T(8,128)(2,1)} %nk_hbm.1, bf16[64,256]{1,0:T(8,128)(2,1)} %nv_hbm.1, bf16[256,256]{1,0:T(8,128)(2,1)} %ck_hbm.1, bf16[256,256]{1,0:T(8,128)(2,1)} %cv_hbm.1, ...), custom_call_target="tpu_custom_call" | custom-call | tf_op jit(solution)/shard_map/pallas_call | solution.py:549
  187.6 1.6 copy.15

commit v4 on v3

--- a/solution.py
+++ b/solution.py
@@ -27,7 +27,7 @@
     ck_hbm,
     cv_hbm,
     table_hbm,
-    gain_ref,
+    gain_hbm,
     wg_hbm,
     wu_hbm,
     wd_hbm,
@@ -39,6 +39,7 @@
     cbuf,
     table,
     found,
+    gain_ref,
     tok_ref,
     m_ref,
     l_ref,
@@ -115,9 +116,7 @@
         )
     local.append(pltpu.make_async_copy(q_hbm.at[:, qcol], qbuf.at[0], loc_sem.at[4]))
     local.append(pltpu.make_async_copy(table_hbm, table, loc_sem.at[5]))
-    for cp in local:
-        cp.start()
-
+    local.append(pltpu.make_async_copy(gain_hbm, gain_ref, loc_sem.at[6]))
     barrier = pltpu.get_barrier_semaphore()
     others = []
     for d in range(nx):
@@ -133,6 +132,8 @@
             device_id={"ctx": z * 2 + (c + k) % 2, "exp": (x + d) % nx},
             device_id_type=MESH,
         )
+    for cp in local:
+        cp.start()
     pl.semaphore_wait(barrier, 2 + len(others))
 
     swap = []
@@ -193,6 +194,7 @@
     o_ref[...] = jnp.zeros_like(o_ref)
     scale = 1.0 / math.sqrt(HEAD)
     local[5].wait()
+    local[6].wait()
     one_row = lax.broadcasted_iota(jnp.int32, (1, HEAD), 1)
 
     def look_up(t, carry):
@@ -304,7 +306,7 @@
 
     there = ([], [])
     for h in range(2):
-        for d, k in others:
+        for d, k in sorted(others, key=lambda o: -min(o[0], nx - o[0])):
             e = (x + d) % nx
             there[h].append(
                 remote(
@@ -404,10 +406,12 @@
 
     lax.fori_loop(0, pairs - 1, row_pair, 0)
     tail = pairs - 1
+    pieces = list(range(8)) if tail > 0 else []
+    for i in pieces[:1]:
+        dense(tail - 1, i)
     for i in row_step(half - 1, True):
-        if i == 1 and tail > 0:
-            for piece in range(8):
-                dense(tail - 1, piece)
+        for piece in (pieces[1:2], pieces[2:], [], [])[i]:
+            dense(tail - 1, piece)
     for q in range(2):
         for d in (0, 1):
             row_copy(d, 2 * d + q, half, 2 * half - 1).wait_recv()
@@ -549,7 +553,7 @@
     return pl.pallas_call(
         functools.partial(layer_kernel, nz, nx),
         out_shape=jax.ShapeDtypeStruct(queries.shape, BF16),
-        in_specs=[vmem, smem] + [hbm] * 6 + [vmem] + [hbm] * 3,
+        in_specs=[vmem, smem] + [hbm] * 10,
         out_specs=vmem,
         scratch_shapes=[
             pltpu.VMEM((nz, 2, span, HEAD), BF16),
@@ -559,6 +563,7 @@
             pltpu.VMEM((2, T, nx * cap), BF16),
             pltpu.VMEM((expert_table.shape[0] // HEAD, HEAD), jnp.int32),
             pltpu.VMEM((T, HEAD), jnp.int32),
+            pltpu.VMEM((1, width), F32),
             pltpu.VMEM((1, lanes), jnp.int32),
             pltpu.VMEM((1, lanes), F32),
             pltpu.VMEM((1, lanes), F32),
@@ -576,7 +581,7 @@
             pltpu.VMEM((2, ff, width), BF16),
             pltpu.VMEM((2, ff, width), BF16),
             pltpu.VMEM((2,) + w_down.shape[1:], BF16),
-            dma((6,)),
+            dma((7,)),
             dma((6,)),
             dma((6,)),
             dma((3,)),

time: 189 us -> 189 us (level)
  no operation moved by 1% of the time
where the time goes in v4:
time: 189 us
  Pallas kernels  187 us (99%)
    pallas_call x1, Pallas kernels, on_device(): pl.pallas_call(functools.partial(layer_kernel, nz, nx), out_shape=jax.Sha...  187 us

profile of v4, /device:TPU:40, one launch (start us, length us, event | category | flops | bytes accessed | tf_op | source)
XLA Modules:
  0.0 188.8 jit_solution(5571757999887216416)
XLA Ops:
  0.7 186.6 %shard_map.118 = bf16[64,1024]{1,0:T(8,128)(2,1)} custom-call(s32[1,1]{1,0:T(1,128)} %bitcast.5.offset_ref, s32[64]{0:T(128)} %ids_ref.1, bf16[64,1024]{1,0:T(8,128)(2,1)} %q_hbm.1, bf16[64,256]{1,0:T(8,128)(2,1)} %nk_hbm.1, bf16[64,256]{1,0:T(8,128)(2,1)} %nv_hbm.1, bf16[256,256]{1,0:T(8,128)(2,1)} %ck_hbm.1, bf16[256,256]{1,0:T(8,128)(2,1)} %cv_hbm.1, ...), custom_call_target="tpu_custom_call" | custom-call | tf_op jit(solution)/shard_map/pallas_call | solution.py:553
  187.2 1.6 copy.15
